TPU v7x, 32 devices: a whole 2x2x4 slice. The times are simulated.
32 devices in a mesh: seq: 16 (over z, x, core), head: 2 (over y).
Axes of the slice: x: 2, y: 2, z: 4, core: 2. Of those that a mesh axis runs over, the one named last changes fastest.
Arguments:
- hidden: bfloat16 [4608, 8192], P('seq'), may hold values from -6 to 6
- norm_gain: bfloat16 [8192], replicated, may hold values from 0.099609375 to 1.8984375
- w_query: bfloat16 [8192, 1024], P('seq', 'head'), may hold values from -0.125 to 0.125
- w_key: bfloat16 [8192, 256], P('seq', 'head'), may hold values from -0.125 to 0.125
- w_value: bfloat16 [8192, 256], P('seq', 'head'), may hold values from -0.0625 to 0.0625
- bias_query: bfloat16 [1024], P('head'), may hold values from -3 to 3
- bias_key: bfloat16 [256], P('head'), may hold values from -200 to 200
- bias_value: bfloat16 [256], P('head'), may hold values from -3 to 3
- w_out: bfloat16 [1024, 8192], P('head', 'seq'), may hold values from -0.1875 to 0.1875
Outputs:
- attn_out: bfloat16 [4608, 8192], P(('seq', 'head'))
All inputs are finite; a program needn't handle non-finite values.
Results may differ from a plain program's by a relative error of at most 0.014.
The roundings to bfloat16 on the way count: a program that leaves them out, or rounds other values in their place, can miss the bound.
Values may be sent and summed in bfloat16 or wider, within the bound.
A program may use at most 192 MiB of HBM per device.

v0:
```python
import jax
import jax.numpy as jnp
from jax import lax
from jax.sharding import PartitionSpec as P

HEAD_DIM = 128


ROPE_BASE = 1000000.0
EPSILON = 1e-06


def rotary(values, positions):
    half_dim = values.shape[-1] // 2
    freq = ROPE_BASE ** (-2.0 * jnp.arange(half_dim, dtype=jnp.float32) / values.shape[-1])
    angles = positions.astype(jnp.float32)[:, None, None] * freq[None, None, :]
    cosine = jnp.cos(angles)
    sine = jnp.sin(angles)
    first = values[..., :half_dim]
    second = values[..., half_dim:]
    return jnp.concatenate(
        [first * cosine - second * sine, second * cosine + first * sine], axis=-1
    )


def local(hidden, norm_gain, w_query, w_key, w_value, bias_query, bias_key, bias_value, w_out):
    row_count = hidden.shape[0]
    head_count = w_query.shape[1] // HEAD_DIM
    first_row = lax.axis_index("seq") * row_count
    last_row = first_row + row_count - 1
    positions = first_row + jnp.arange(row_count, dtype=jnp.int32)
    widened = hidden.astype(jnp.float32)
    inverse = lax.rsqrt(jnp.mean(widened * widened, axis=-1, keepdims=True) + EPSILON)
    normed = (widened * inverse * norm_gain.astype(jnp.float32)).astype(jnp.bfloat16)
    query = jnp.dot(
        normed,
        lax.all_gather(w_query, "seq", axis=0, tiled=True),
        preferred_element_type=jnp.float32,
    )
    keys = jnp.dot(
        normed, lax.all_gather(w_key, "seq", axis=0, tiled=True), preferred_element_type=jnp.float32
    )
    values = jnp.dot(
        normed,
        lax.all_gather(w_value, "seq", axis=0, tiled=True),
        preferred_element_type=jnp.float32,
    )
    query = query + bias_query.astype(jnp.float32)
    keys = keys + bias_key.astype(jnp.float32)
    values = values + bias_value.astype(jnp.float32)
    query = rotary(query.reshape(row_count, head_count, HEAD_DIM), positions).astype(jnp.bfloat16)
    keys = (
        rotary(keys.reshape(row_count, 1, HEAD_DIM), positions)
        .reshape(row_count, HEAD_DIM)
        .astype(jnp.bfloat16)
    )
    values = values.astype(jnp.bfloat16)
    query_heads = query.transpose(1, 0, 2)
    scaling = HEAD_DIM ** (-0.5)
    initial = (
        jnp.full((head_count, row_count), -1e30, jnp.float32),
        jnp.zeros((head_count, row_count), jnp.float32),
        jnp.zeros((head_count, row_count, HEAD_DIM), jnp.float32),
    )
    key_piece = lax.all_gather(keys, "seq", axis=0, tiled=True)
    value_piece = lax.all_gather(values, "seq", axis=0, tiled=True)

    def update(state):
        highest, total, summed = state
        scores = (
            jnp.einsum("hqd,kd->hqk", query_heads, key_piece, preferred_element_type=jnp.float32)
            * scaling
        )
        key_positions = jnp.arange(key_piece.shape[0], dtype=jnp.int32)
        allowed = positions[:, None] >= key_positions[None, :]
        scores = jnp.where(allowed[None], scores, -jnp.inf)
        new_high = jnp.maximum(highest, jnp.max(scores, axis=-1))
        probs = jnp.exp(scores - new_high[..., None])
        total = jnp.sum(probs, axis=-1)
        mixed = jnp.einsum(
            "hqk,kd->hqd",
            probs.astype(jnp.bfloat16),
            value_piece,
            preferred_element_type=jnp.float32,
        )
        return (new_high, total, mixed)

    def unchanged(state):
        return state

    highest, total, summed = lax.cond(jnp.int32(0) <= last_row, update, unchanged, initial)
    attended = (summed / total[..., None]).astype(jnp.bfloat16)
    attended = attended.transpose(1, 0, 2).reshape(row_count, head_count * HEAD_DIM)
    partial_out = jnp.dot(
        attended,
        lax.all_gather(w_out, "seq", axis=1, tiled=True),
        preferred_element_type=jnp.float32,
    )
    result = lax.psum_scatter(
        partial_out.astype(jnp.bfloat16), "head", scatter_dimension=0, tiled=True
    )
    return result


def solution(mesh):
    in_specs = (
        P("seq", None),
        P(),
        P("seq", "head"),
        P("seq", "head"),
        P("seq", "head"),
        P("head"),
        P("head"),
        P("head"),
        P("head", "seq"),
    )
    out_specs = P(("seq", "head"), None)
    return jax.shard_map(local, mesh=mesh, in_specs=in_specs, out_specs=out_specs, check_vma=False)
```

profile of v0, /device:TPU:18, one launch (start us, length us, event | category | flops | bytes accessed | tf_op | source)
XLA Modules:
  0.0 399.6 jit_solution(17232137514900571910)
XLA Ops:
  6.5 0.7 all-gather.10.cloned.1.call-update
  7.3 0.7 all-gather.12.cloned.1.call-update
  8.1 0.7 all-gather.8.cloned.1.call-update
  8.8 0.7 convert_element_type.48
  9.5 0.7 convert_element_type.52
  10.2 3.4 fusion.11
  13.6 35.8 %all-gather.10.cloned.1.call-done = bf16[8192,128]{1,0:T(8,128)(2,1)} async-done(((bf16[512,128]{1,0:T(8,128)(2,1)}), bf16[8192,128]{1,0:T(8,128)(2,1)}) %all-gather.10.cloned.1.call-update) | async-done | bytes 2097168 | tf_op jit(solution)/shard_map/all_gather | solution.py:41
  49.3 4.6 %fusion.14 = f32[288,1,128]{2,0,1:T(8,128)S(1)} fusion(bf16[8192,128]{1,0:T(8,128)(2,1)} %all-gather.10.cloned.1.call-done, f32[128]{0:T(128)S(1)} %convert_element_type.52, bf16[288,8192]{1,0:T(8,128)(2,1)} %param.11, f32[8192]{0:T(1024)S(1)} %convert_element_type.48, f32[288]{0:T(512)S(1)} %add_rsqrt_fusion), kind=kOutput, calls=%fused_computation.24 | convolution fusion | flops 613453824 | bytes 6997632 | tf_op jit(solution)/shard_map/dot_general | solution.py:40
  53.9 0.6 fusion.24
  54.5 0.7 pad_maximum_fusion
  55.3 0.0 all-gather.14.cloned.1.call-start
  55.4 36.3 %all-gather.12.cloned.1.call-done = bf16[8192,128]{1,0:T(8,128)(2,1)} async-done(((bf16[512,128]{1,0:T(8,128)(2,1)}), bf16[8192,128]{1,0:T(8,128)(2,1)}) %all-gather.12.cloned.1.call-update) | async-done | bytes 2097168 | tf_op jit(solution)/shard_map/all_gather | solution.py:45
  91.7 5.1 %fusion.15 = bf16[288,128]{1,0:T(8,128)(2,1)} fusion(bf16[8192,128]{1,0:T(8,128)(2,1)} %all-gather.12.cloned.1.call-done, f32[128]{0:T(128)S(1)} %convert_element_type.54, bf16[288,8192]{1,0:T(8,128)(2,1)} %param.11, f32[8192]{0:T(1024)S(1)} %convert_element_type.48, f32[288]{0:T(512)S(1)} %add_rsqrt_fusion), kind=kOutput, calls=%fused_computation.25 | convolution fusion | flops 613490688 | bytes 6923904 | tf_op jit(solution)/shard_map/dot_general | solution.py:43
  96.9 0.5 all-gather.16.cloned.1.call-update
  97.4 0.2 reduce-scatter.2.cloned.1.call-start
  97.7 0.6 multiply_cosine_fusion.1
  98.3 69.9 %all-gather.8.cloned.1.call-done = bf16[8192,512]{1,0:T(8,128)(2,1)} async-done(((bf16[512,512]{1,0:T(8,128)(2,1)}), bf16[8192,512]{1,0:T(8,128)(2,1)}) %all-gather.8.cloned.1.call-update) | async-done | bytes 8388624 | tf_op jit(solution)/shard_map/all_gather | solution.py:37
  168.1 7.0 %convolution_add_fusion = f32[288,512]{1,0:T(8,128)S(1)} fusion(bf16[8192,512]{1,0:T(8,128)(2,1)} %all-gather.8.cloned.1.call-done, f32[512]{0:T(512)S(1)} %convert_element_type.50, bf16[288,8192]{1,0:T(8,128)(2,1)} %param.11, f32[8192]{0:T(1024)S(1)} %convert_element_type.48, f32[288]{0:T(512)S(1)} %add_rsqrt_fusion), kind=kOutput, calls=%fused_computation.21 | convolution fusion | flops 2425503744 | bytes 13732992 | tf_op jit(solution)/shard_map/dot_general | solution.py:35
  175.2 0.2 reshape.159
  175.4 0.4 fusion.30
  175.7 0.2 subtract_convert_fusion
  175.9 0.2 maximum_bitcast_fusion
  176.1 30.4 %all-gather.18.cloned.1.call-done = bf16[4608,1,128]{2,0,1:T(8,128)(2,1)} async-done(((bf16[288,1,128]{2,0,1:T(8,128)(2,1)}), bf16[4608,1,128]{2,0,1:T(8,128)(2,1)}) %all-gather.18.cloned.1.call-update) | async-done | bytes 1179664 | tf_op jit(solution)/shard_map/all_gather | solution.py:65
  206.5 39.3 %all-gather.14.cloned.1.call-done = bf16[4608,128]{1,0:T(8,128)(2,1)} async-done(((bf16[288,128]{1,0:T(8,128)(2,1)}), bf16[4608,128]{1,0:T(8,128)(2,1)}) %all-gather.14.cloned.1.call-update) | async-done | bytes 1179664 | tf_op jit(solution)/shard_map/all_gather | solution.py:66
  245.8 19.5 %conditional.1 = (f32[4,288]{1,0:T(4,128)S(1)}, f32[4,288,128]{2,1,0:T(8,128)S(1)}) conditional(s32[]{:T(128)} %convert_element_type.46, () %tuple.13, (s32[]{:T(128)}, s32[288]{0:T(512)S(1)}, bf16[4,288,128]{2,1,0:T(8,128)(2,1)S(1)}, bf16[4608,128]{1,0:T(8,128)(2,1)}, bf16[4608,128]{1,0:T(8,128)(2,1)}) %tuple.36), branch_computations={%region_1.0_spmd, %region_2.5_spmd} | conditional | flops 2777627648 | bytes 72284560 | solution.py:91
  245.8 0.8 iota_compare_fusion
  246.6 5.5 %fusion = (f32[4,288]{1,0:T(4,128)S(1)}, f32[4,288,4608]{2,1,0:T(8,128)S(1)}) fusion(pred[288,4608]{1,0:T(8,128)(4,1)S(1)} %iota_compare_fusion, bf16[4,288,128]{2,1,0:T(8,128)(2,1)S(1)} %get-tuple-element.19, bf16[4608,128]{1,0:T(8,128)(2,1)} %get-tuple-element.20), kind=kOutput, calls=%fused_computation.2 | convolution fusion | flops 1374878592 | bytes 24039936 | tf_op jit(solution)/shard_map/cond/branch_1_fun/hqd,kd->hqk/dot_general | solution.py:71
  252.1 6.6 %fusion.3 = f32[4,288,128]{2,1,0:T(8,128)S(1)} fusion(f32[4,288,4608]{2,1,0:T(8,128)S(1)} %get-tuple-element.27, f32[4,288]{1,0:T(4,128)S(1)} %broadcast_maximum_fusion, pred[288,4608]{1,0:T(8,128)(4,1)S(1)} %iota_compare_fusion, bf16[4608,128]{1,0:T(8,128)(2,1)} %get-tuple-element.21), kind=kOutput, calls=%fused_computation.5 | convolution fusion | flops 1380188160 | bytes 24334848 | tf_op jit(solution)/shard_map/cond/branch_1_fun/hqk,kd->hqd/dot_general | solution.py:80
  258.7 6.6 %fusion.2 = f32[4,288]{1,0:T(4,128)S(1)} fusion(f32[4,288,4608]{2,1,0:T(8,128)S(1)} %get-tuple-element.27, f32[4,288]{1,0:T(4,128)S(1)} %broadcast_maximum_fusion, pred[288,4608]{1,0:T(8,128)(4,1)S(1)} %iota_compare_fusion), kind=kLoop, calls=%fused_computation.4 | loop fusion | flops 21232512 | bytes 22569984 | tf_op jit(solution)/shard_map/cond/branch_1_fun/reduce_sum | solution.py:79
  265.3 59.5 %all-gather.16.cloned.1.call-done = bf16[512,8192]{1,0:T(8,128)(2,1)} async-done(((bf16[512,512]{1,0:T(8,128)(2,1)}), bf16[512,8192]{1,0:T(8,128)(2,1)}) %all-gather.16.cloned.1.call-update) | async-done | bytes 8388624 | tf_op jit(solution)/shard_map/all_gather | solution.py:96
  324.8 7.7 %convolution_convert_fusion = bf16[288,8192]{1,0:T(8,128)(2,1)} fusion(bf16[512,8192]{1,0:T(8,128)(2,1)} %all-gather.16.cloned.1.call-done, f32[4,288,128]{2,1,0:T(8,128)S(1)} %get-tuple-element.24, f32[4,288]{1,0:T(4,128)S(1)} %get-tuple-element.25), kind=kOutput, calls=%fused_computation.17 | convolution fusion | flops 2418573312 | bytes 13701632 | tf_op jit(solution)/shard_map/dot_general | solution.py:94
  332.6 60.2 %reduce-scatter.2.cloned.1.call-done = bf16[144,8192]{1,0:T(8,128)(2,1)} async-done(((bf16[288,8192]{1,0:T(8,128)(2,1)}), bf16[144,8192]{1,0:T(8,128)(2,1)}) %reduce-scatter.2.cloned.1.call-update) | async-done | bytes 2359312 | tf_op jit(solution)/shard_map/reduce_scatter | solution.py:99
  (20 shorter events, 0.3 us)
Async XLA Ops:
  6.5 42.8 %all-gather.10.cloned.1.call-start = ((), (), s32[]{:S(2)}) async-start(), calls=%async_computation.2 | async-start | bytes 2228224 | tf_op jit(solution)/shard_map/all_gather | solution.py:41
  7.3 84.4 %all-gather.12.cloned.1.call-start = ((), (), s32[]{:S(2)}) async-start(), calls=%async_computation.3 | async-start | bytes 2228224 | tf_op jit(solution)/shard_map/all_gather | solution.py:45
  8.0 160.1 %all-gather.8.cloned.1.call-start = ((), (), s32[]{:S(2)}) async-start(), calls=%async_computation.1 | async-start | bytes 8912896 | tf_op jit(solution)/shard_map/all_gather | solution.py:37
  8.7 197.7 %all-gather.18.cloned.1.call-start = ((), (), s32[]{:S(2)}) async-start(), calls=%async_computation.7 | async-start | bytes 1253376 | tf_op jit(solution)/shard_map/all_gather | solution.py:65
  13.5 41.8 %copy-start.1 = (bf16[128]{0:T(256)(128)(2,1)S(1)}, bf16[128]{0:T(256)(128)(2,1)}, u32[]{:S(2)}) copy-start(bf16[128]{0:T(256)(128)(2,1)} %param.18) | copy-start | bytes 772
  53.9 43.8 %copy-start = (bf16[512]{0:T(512)(128)(2,1)S(1)}, bf16[512]{0:T(512)(128)(2,1)}, u32[]{:S(2)}) copy-start(bf16[512]{0:T(512)(128)(2,1)} %param.16) | copy-start | bytes 3076
  55.3 190.5 %all-gather.14.cloned.1.call-start = ((), (), s32[]{:S(2)}) async-start(), calls=%async_computation.4 | async-start | bytes 1253376 | tf_op jit(solution)/shard_map/all_gather | solution.py:66
  96.9 228.0 %all-gather.16.cloned.1.call-start = ((), (), s32[]{:S(2)}) async-start(), calls=%async_computation.5 | async-start | bytes 8912896 | tf_op jit(solution)/shard_map/all_gather | solution.py:96
  97.4 295.3 %reduce-scatter.2.cloned.1.call-start = ((), (), s32[]{:S(2)}) async-start(), calls=%async_computation.6 | async-start | bytes 7077888 | tf_op jit(solution)/shard_map/reduce_scatter | solution.py:99
Sparse Core Ops, SparseCore 0:
  9.5 39.7 all-gather.9
  51.5 40.1 all-gather.11
  93.8 74.2 all-gather.7
  170.3 36.1 all-gather.17
  208.6 37.1 all-gather.13
  247.8 76.9 all-gather.15
  332.7 60.0 reduce-scatter.1
where the time goes:
time: 402 us; the launch traced here: 400 us
  waiting for transfers between devices  334 us (83%)
  matrix products  36.6 us (9%)
  other arithmetic  14.4 us (4%)
  between operations  13.6 us (3%)
    all_gather x1, waiting for transfers between devices, local(): lax.all_gather(w_query, 'seq', axis=0, tiled=True)  69.9 us
    reduce_scatter x1, waiting for transfers between devices, local(): lax.psum_scatter(partial_out.astype(jnp.bfloat16), 'head', scatter_dimens...  60.2 us
    all_gather x1, waiting for transfers between devices, local(): lax.all_gather(w_out, 'seq', axis=1, tiled=True)  59.5 us
    all_gather x1, waiting for transfers between devices, local(): value_piece = lax.all_gather(values, 'seq', axis=0, tiled=True)  39.3 us
    all_gather x1, waiting for transfers between devices, local(): lax.all_gather(w_value, 'seq', axis=0, tiled=True)  36.3 us
    all_gather x1, waiting for transfers between devices, local(): lax.all_gather(w_key, 'seq', axis=0, tiled=True)  35.8 us
    all_gather x1, waiting for transfers between devices, local(): key_piece = lax.all_gather(keys, 'seq', axis=0, tiled=True)  30.4 us
  transfers between devices with their start and end apart: 7, of which 7 were waited for; matrix products, arithmetic and copies ran while one was open for 11% of the time, Pallas kernels for 0%

commit v1 on v0

v1 whole, which is shorter than its diff:
```python
import functools

import jax
import jax.numpy as jnp
from jax import lax
from jax.experimental import pallas as pl
from jax.experimental.pallas import tpu as pltpu
from jax.sharding import PartitionSpec as P

HEAD_DIM = 128
ROPE_BASE = 1000000.0
EPSILON = 1e-06
MESH = pl.DeviceIdType.MESH
F32 = jnp.float32
BF16 = jnp.bfloat16


def kernel(
    n, groups, exchange,
    hidden, w_query, w_key, w_value, w_out, gain, bias, cosine, sine,
    out,
    hid, normed, w_all, wo_all, acc, kv_all, q_ref, high, total, mixed, att, ts, tr, tm,
    load_sem, ws, wr, wps, wpr, os_, or_, ops, opr, ks, kr, kps, kpr, ys, yr,
):
    chips = n // 2
    depth = chips // 2
    me = lax.axis_index("seq")
    group = lax.axis_index("head")
    core = me % 2
    chip = me // 2
    ring = chip // 2 + (chip % 2) * (2 * depth - 1 - 2 * (chip // 2))

    def device_at(position, which):
        position = (position + 2 * chips) % chips
        side = position // depth
        row = position + side * (2 * depth - 1 - 2 * position)
        return 2 * (2 * row + side) + which

    right = device_at(ring + 1, core)
    left = device_at(ring - 1, core)
    partner = 2 * chip + (1 - core)
    neighbours = (right, left)

    def source_at(direction, offset, which):
        return device_at(ring - offset if direction == 0 else ring + offset, which)

    rows, width = hidden.shape
    half_depth = w_query.shape[0] // 2
    q_cols = w_query.shape[1]
    heads = q_cols // HEAD_DIM
    half_cols = w_out.shape[1] // 2
    rh = rows // groups

    loads = [pltpu.make_async_copy(hidden, hid, load_sem.at[0])]
    for h in range(2):
        span = pl.ds(h * half_depth, half_depth)
        slot = w_all.at[2 * me + h]
        loads.append(pltpu.make_async_copy(w_query.at[span], slot.at[:, pl.ds(0, q_cols)], load_sem.at[1 + 4 * h]))
        loads.append(pltpu.make_async_copy(w_key.at[span], slot.at[:, pl.ds(q_cols, HEAD_DIM)], load_sem.at[2 + 4 * h]))
        loads.append(pltpu.make_async_copy(w_value.at[span], slot.at[:, pl.ds(q_cols + HEAD_DIM, HEAD_DIM)], load_sem.at[3 + 4 * h]))
        loads.append(pltpu.make_async_copy(w_out.at[:, pl.ds(h * half_cols, half_cols)], wo_all.at[2 * me + h], load_sem.at[4 + 4 * h]))
    for copy in loads:
        copy.start()

    barrier = pltpu.get_barrier_semaphore()
    for device in (right, left, partner):
        pl.semaphore_signal(barrier, inc=1, device_id={"seq": device}, device_id_type=MESH)
    peers = range(1, groups) if exchange else ()
    for p in peers:
        pl.semaphore_signal(barrier, inc=1, device_id={"head": (group + p) % groups}, device_id_type=MESH)
    pl.semaphore_wait(barrier, 3 + len(peers))

    def remote(ref, send, recv, key, device):
        return pltpu.make_async_remote_copy(
            src_ref=ref, dst_ref=ref, send_sem=send.at[key], recv_sem=recv.at[key],
            device_id={"seq": device}, device_id_type=MESH,
        )

    def piece(buffer, index, j):
        size = buffer.shape[1] // 2
        return buffer.at[index, pl.ds(j * size, size)]

    def key_of(direction, step, j):
        return (direction * chips + step) * 2 + j

    def ring_begin(buffer, sems):
        ss, rs, pss, prs = sems
        for j in range(2):
            for d in range(2):
                own = piece(buffer, 2 * me + d, j)
                remote(own, ss, rs, key_of(d, 0, j), neighbours[d]).start()
        for j in range(2):
            for d in range(2):
                own = piece(buffer, 2 * me + d, j)
                remote(own, pss, prs, key_of(d, chips - 1, j), partner).start()

    def ring_advance(buffer, sems, t):
        ss, rs, pss, prs = sems

        @pl.when(t < chips - 1)
        def _():
            for j in range(2):
                for d in range(2):
                    block = piece(buffer, 2 * source_at(d, t + 1, core) + d, j)
                    remote(block, ss, rs, key_of(d, t, j), neighbours[d]).wait_recv()

                    @pl.when(t < chips - 2)
                    def _():
                        remote(block, ss, rs, key_of(d, t + 1, j), neighbours[d]).start()

                    remote(block, pss, prs, key_of(d, t, j), partner).start()

    def partner_wait(buffer, sems, t):
        ss, rs, pss, prs = sems
        for j in range(2):
            for d in range(2):
                block = piece(buffer, 2 * source_at(d, t, 1 - core) + d, j)
                remote(block, pss, prs, key_of(d, (t + chips - 1) % chips, j), partner).wait_recv()

    def ring_drain(buffer, sems):
        ss, rs, pss, prs = sems

        def body(t, carry):
            for j in range(2):
                for d in range(2):
                    block = piece(buffer, 2 * me + d, j)

                    @pl.when(t < chips - 1)
                    def _():
                        remote(block, ss, rs, key_of(d, t, j), neighbours[d]).wait_send()

                    remote(block, pss, prs, key_of(d, t, j), partner).wait_send()
            return carry

        lax.fori_loop(0, chips, body, 0)

    w_sems = (ws, wr, wps, wpr)
    o_sems = (os_, or_, ops, opr)

    for copy in loads[1:]:
        copy.wait()
    ring_begin(w_all, w_sems)
    loads[0].wait()
    slices = 2 * n
    step_cols = width // slices

    def columns(i):
        return pl.ds(pl.multiple_of(i * step_cols, step_cols), step_cols)

    def square(i, carry):
        x = hid[:, columns(i)].astype(F32)
        return carry + x * x

    squares = lax.fori_loop(0, slices, square, jnp.zeros((rows, step_cols), F32))
    inverse = lax.rsqrt(jnp.sum(squares, axis=-1, keepdims=True) * (1.0 / width) + EPSILON)

    def normalise(i, carry):
        x = hid[:, columns(i)].astype(F32)
        normed[i] = (x * inverse * gain[i]).astype(BF16)
        return carry

    lax.fori_loop(0, slices, normalise, 0)
    acc[...] = jnp.broadcast_to(bias[...], acc.shape)

    def project(t, carry):
        ring_advance(w_all, w_sems, t)
        partner_wait(w_all, w_sems, t)
        for d in range(2):
            i = 2 * source_at(d, t, core) + d
            k = 2 * source_at(d, t, 1 - core) + d
            acc[...] += jnp.dot(normed[i], w_all[i], preferred_element_type=F32) + jnp.dot(
                normed[k], w_all[k], preferred_element_type=F32
            )
        return carry

    lax.fori_loop(0, chips, project, 0)

    def rotary(x):
        return x * cosine[...] + pltpu.roll(x, HEAD_DIM // 2, 1) * sine[...]

    kv_all[me, :, pl.ds(0, HEAD_DIM)] = rotary(acc[:, pl.ds(q_cols, HEAD_DIM)]).astype(BF16)
    kv_all[me, :, pl.ds(HEAD_DIM, HEAD_DIM)] = acc[:, pl.ds(q_cols + HEAD_DIM, HEAD_DIM)].astype(BF16)
    for h in range(heads):
        q_ref[h] = rotary(acc[:, pl.ds(h * HEAD_DIM, HEAD_DIM)]).astype(BF16)

    reach = (chips // 2, chips - 1 - chips // 2)

    def kv_copy(owner, ss, rs, direction, step, device):
        return remote(kv_all.at[owner], ss, rs, direction * chips + step, device)

    for d in range(2):
        kv_copy(me, ks, kr, d, 0, neighbours[d]).start()
    kv_copy(me, kps, kpr, 0, chips - 1, partner).start()

    scaling = HEAD_DIM ** (-0.5)

    def attend(b, first, diagonal):
        for h in range(heads):
            scores = lax.dot_general(
                q_ref[h], kv_all[b, :, pl.ds(0, HEAD_DIM)], (((1,), (1,)), ((), ())),
                preferred_element_type=F32,
            ) * scaling
            if diagonal:
                row = lax.broadcasted_iota(jnp.int32, scores.shape, 0)
                col = lax.broadcasted_iota(jnp.int32, scores.shape, 1)
                scores = jnp.where(row >= col, scores, -jnp.inf)
            top = jnp.max(scores, axis=-1, keepdims=True)
            if not first:
                old = high[h]
                top = jnp.maximum(old, top)
            probs = jnp.exp(scores - top)
            part = jnp.sum(probs, axis=-1, keepdims=True)
            product = jnp.dot(
                probs.astype(BF16), kv_all[b, :, pl.ds(HEAD_DIM, HEAD_DIM)], preferred_element_type=F32
            )
            if not first:
                shrink = jnp.exp(old - top)
                part = part + total[h] * shrink
                product = product + mixed[h] * shrink
            high[h] = top
            total[h] = part
            mixed[h] = product

    attend(me, True, True)

    def attend_earlier(b):
        @pl.when(b < me)
        def _():
            attend(b, False, False)

    def attention(t, carry):
        for d in range(2):
            @pl.when(t < reach[d])
            def _():
                owner = source_at(d, t + 1, core)
                kv_copy(owner, ks, kr, d, t, neighbours[d]).wait_recv()

                @pl.when(t + 1 < reach[d])
                def _():
                    kv_copy(owner, ks, kr, d, t + 1, neighbours[d]).start()

                kv_copy(owner, kps, kpr, d, t, partner).start()

        @pl.when(t == 0)
        def _():
            kv_copy(partner, kps, kpr, 0, chips - 1, partner).wait_recv()
            attend_earlier(partner)

        for d in range(2):
            @pl.when((t > 0) & (t <= reach[d]))
            def _():
                attend_earlier(source_at(d, t, core))
                owner = source_at(d, t, 1 - core)
                kv_copy(owner, kps, kpr, d, t - 1, partner).wait_recv()
                attend_earlier(owner)
        return carry

    lax.fori_loop(0, reach[0] + 1, attention, 0)
    ring_begin(wo_all, o_sems)
    for h in range(heads):
        att[:, pl.ds(h * HEAD_DIM, HEAD_DIM)] = (mixed[h] / total[h]).astype(BF16)

    def term_copy(p, i):
        return pltpu.make_async_remote_copy(
            src_ref=ts.at[p - 1, i], dst_ref=tr.at[p - 1, i],
            send_sem=ys.at[(p - 1) * slices + i], recv_sem=yr.at[(p - 1) * slices + i],
            device_id={"head": (group + p) % groups}, device_id_type=MESH,
        )

    def out_columns(i):
        return pl.ds(pl.multiple_of(i * half_cols, half_cols), half_cols)

    def make_term(i):
        if not exchange:
            out[:, out_columns(i)] = jnp.dot(att[...], wo_all[i], preferred_element_type=F32).astype(BF16)
            return
        for p in peers:
            span = pl.ds(pl.multiple_of(((group + p) % groups) * rh, rh), rh)
            ts[p - 1, i] = jnp.dot(att[span, :], wo_all[i], preferred_element_type=F32).astype(BF16)
            term_copy(p, i).start()
        span = pl.ds(pl.multiple_of(group * rh, rh), rh)
        tm[i] = jnp.dot(att[span, :], wo_all[i], preferred_element_type=F32).astype(BF16)

    def blocks_of(t):
        return [2 * source_at(d, t, which) + d for d in range(2) for which in (core, 1 - core)]

    def project_out(t, carry):
        ring_advance(wo_all, o_sems, t)
        partner_wait(wo_all, o_sems, t)
        for i in blocks_of(t):
            make_term(i)
        return carry

    lax.fori_loop(0, chips, project_out, 0)

    def finish(t, carry):
        for i in blocks_of(t):
            value = tm[i].astype(F32)
            for p in peers:
                term_copy(p, i).wait_recv()
                value = value + tr[p - 1, i].astype(F32)
            out[:, out_columns(i)] = value.astype(BF16)
        return carry

    if exchange:
        lax.fori_loop(0, chips, finish, 0)

        def sent(i, carry):
            for p in peers:
                term_copy(p, i).wait_send()
            return carry

        lax.fori_loop(0, slices, sent, 0)

    ring_drain(w_all, w_sems)
    ring_drain(wo_all, o_sems)
    for d in range(2):
        for t in range(reach[d]):
            kv_copy(me, ks, kr, d, t, neighbours[d]).wait_send()
            kv_copy(me, kps, kpr, d, t, partner).wait_send()
    kv_copy(me, kps, kpr, 0, chips - 1, partner).wait_send()


def local(n, groups, hidden, norm_gain, w_query, w_key, w_value, bias_query, bias_key, bias_value, w_out):
    rows, width = hidden.shape
    cols = w_query.shape[1]
    heads = cols // HEAD_DIM
    wide = cols + 2 * HEAD_DIM
    chips = n // 2
    exchange = groups > 1 and (rows // groups) % 16 == 0
    rh = rows // groups
    slices = 2 * n
    half_depth = w_query.shape[0] // 2
    half_cols = w_out.shape[1] // 2

    positions = lax.axis_index("seq") * rows + jnp.arange(rows, dtype=jnp.int32)
    freq = ROPE_BASE ** (-2.0 * jnp.arange(HEAD_DIM // 2, dtype=F32) / HEAD_DIM)
    angles = positions.astype(F32)[:, None] * freq[None, :]
    cosine = jnp.cos(angles)
    sine = jnp.sin(angles)
    cosine = jnp.concatenate([cosine, cosine], axis=-1)
    sine = jnp.concatenate([-sine, sine], axis=-1)
    gain = norm_gain.astype(F32).reshape(slices, 1, width // slices)
    bias = jnp.concatenate([bias_query, bias_key, bias_value]).astype(F32)[None, :]

    any_spec = pl.BlockSpec(memory_space=pl.ANY)
    vmem = pl.BlockSpec(memory_space=pltpu.VMEM)
    links = max(groups - 1, 1) if exchange else 1
    pieces = slices if exchange else 1
    rpart = rh if exchange else 16
    dma = pltpu.SemaphoreType.DMA
    result = pl.pallas_call(
        functools.partial(kernel, n, groups, exchange),
        out_shape=jax.ShapeDtypeStruct((rh if exchange else rows, w_out.shape[1] * n), BF16),
        in_specs=[any_spec] * 5 + [vmem] * 4,
        out_specs=vmem,
        scratch_shapes=[
            pltpu.VMEM((rows, width), BF16),
            pltpu.VMEM((slices, rows, width // slices), BF16),
            pltpu.VMEM((slices, half_depth, wide), BF16),
            pltpu.VMEM((slices, w_out.shape[0], half_cols), BF16),
            pltpu.VMEM((rows, wide), F32),
            pltpu.VMEM((n, rows, 2 * HEAD_DIM), BF16),
            pltpu.VMEM((heads, rows, HEAD_DIM), BF16),
            pltpu.VMEM((heads, rows, 1), F32),
            pltpu.VMEM((heads, rows, 1), F32),
            pltpu.VMEM((heads, rows, HEAD_DIM), F32),
            pltpu.VMEM((rows, cols), BF16),
            pltpu.VMEM((links, pieces, rpart, half_cols), BF16),
            pltpu.VMEM((links, pieces, rpart, half_cols), BF16),
            pltpu.VMEM((pieces, rpart, half_cols), BF16),
            dma((9,)),
        ]
        + [dma((4 * chips,))] * 8
        + [dma((2 * chips,))] * 4
        + [dma((links * pieces,))] * 2,
        compiler_params=pltpu.CompilerParams(
            collective_id=0, has_side_effects=True, vmem_limit_bytes=64 * 1024 * 1024 - 128 * 1024
        ),
    )(hidden, w_query, w_key, w_value, w_out, gain, bias, cosine, sine)
    if exchange:
        return result
    return lax.psum_scatter(result, "head", scatter_dimension=0, tiled=True)


def solution(mesh):
    in_specs = (
        P("seq", None),
        P(),
        P("seq", "head"),
        P("seq", "head"),
        P("seq", "head"),
        P("head"),
        P("head"),
        P("head"),
        P("head", "seq"),
    )
    out_specs = P(("seq", "head"), None)
    body = functools.partial(local, mesh.shape["seq"], mesh.shape["head"])
    return jax.shard_map(body, mesh=mesh, in_specs=in_specs, out_specs=out_specs, check_vma=False)
```

time: 402 us -> 176 us (0.44)
  waiting for transfers between devices: 334 us -> 0 us
  Pallas kernels: 0 us -> 168 us
  matrix products: 36.6 us -> 0 us
  between operations: 13.6 us -> 0.02 us
  other arithmetic: 14.4 us -> 4.06 us
    all_gather x6 -> x0, waiting for transfers between devices: 271 us -> none  [the longest x1 69.9 us: local(): lax.all_gather(w_query, 'seq', axis=0, tiled=True)]
    pallas_call x0 -> x1, Pallas kernels: none -> 168 us  [local(): pl.pallas_call(functools.partial(kernel, n, groups, exchange), out_shape=...]
    reduce_scatter x1 -> x0, waiting for transfers between devices: 60.2 us -> none  [local(): lax.psum_scatter(partial_out.astype(jnp.bfloat16), 'head', scatter_dimens...]
    dot_general x6 -> x0, matrix products: 36.6 us -> none  [the longest x1 7.72 us: local(): jnp.dot(attended, lax.all_gather(w_out, 'seq', axis=1, tiled=True), prefe...]
    reduce_sum x2 -> x0, other arithmetic: 9.94 us -> none  [the longest x1 6.58 us: update(): total = jnp.sum(probs, axis=-1)]
  transfers between devices with their start and end apart: 7 -> 0, of which waited for: 7 -> 0; matrix products, arithmetic and copies ran while one was open for 11% -> 0% of each run, Pallas kernels for 0% -> 0%
where the time goes in v1:
time: 176 us
  Pallas kernels  168 us (95%)
  other arithmetic  4.06 us (2%)
  local copies, waits for them, and re-layouts  3.96 us (2%)
    pallas_call x1, Pallas kernels, local(): pl.pallas_call(functools.partial(kernel, n, groups, exchange), out_shape=...  168 us

profile of v1, /device:TPU:18, one launch (start us, length us, event | category | flops | bytes accessed | tf_op | source)
XLA Modules:
  0.0 176.2 jit_solution(691864503739303746)
XLA Ops:
  0.0 0.7 concatenate.22
  0.7 1.3 maximum_convert_fusion.bias
  2.0 1.3 reshape.59
  3.3 0.6 fusion
  3.9 0.9 pad_maximum_fusion
  4.8 168.1 %shard_map.91 = bf16[144,8192]{1,0:T(8,128)(2,1)} custom-call(bf16[288,8192]{1,0:T(8,128)(2,1)} %hidden.1, bf16[512,512]{1,0:T(8,128)(2,1)} %w_query.1, bf16[512,128]{1,0:T(8,128)(2,1)} %w_key.1, bf16[512,128]{1,0:T(8,128)(2,1)} %w_value.1, bf16[512,512]{1,0:T(8,128)(2,1)} %w_out.1, f32[32,1,256]{2,1,0:T(1,128)} %bitcast.3, ...), custom_call_target="tpu_custom_call" | custom-call | tf_op jit(solution)/shard_map/pallas_call | solution.py:352
  172.9 3.3 %copy.11 = bf16[144,8192]{1,0:T(8,128)(2,1)} copy(bf16[144,8192]{1,0:T(8,128)(2,1)} %shard_map.91) | data formatting | bytes 4718592
  (2 shorter events, 0.0 us)

commit v2 on v1

--- a/solution.py
+++ b/solution.py
@@ -2,6 +2,7 @@
 
 import jax
 import jax.numpy as jnp
+import numpy as np
 from jax import lax
 from jax.experimental import pallas as pl
 from jax.experimental.pallas import tpu as pltpu
@@ -17,9 +18,10 @@
 
 def kernel(
     n, groups, exchange,
-    hidden, w_query, w_key, w_value, w_out, gain, bias, cosine, sine,
+    hidden, w_query, w_key, w_value, w_out, gain, bias_query, bias_key, bias_value,
+    near_cos, near_sin, far_cos, far_sin,
     out,
-    hid, normed, w_all, wo_all, acc, kv_all, q_ref, high, total, mixed, att, ts, tr, tm,
+    hid, w_all, wo_all, acc, kv_all, q_ref, high, total, mixed, att, ts, tr, tm,
     load_sem, ws, wr, wps, wpr, os_, or_, ops, opr, ks, kr, kps, kpr, ys, yr,
 ):
     chips = n // 2
@@ -154,13 +156,15 @@
     squares = lax.fori_loop(0, slices, square, jnp.zeros((rows, step_cols), F32))
     inverse = lax.rsqrt(jnp.sum(squares, axis=-1, keepdims=True) * (1.0 / width) + EPSILON)
 
-    def normalise(i, carry):
-        x = hid[:, columns(i)].astype(F32)
-        normed[i] = (x * inverse * gain[i]).astype(BF16)
-        return carry
-
-    lax.fori_loop(0, slices, normalise, 0)
-    acc[...] = jnp.broadcast_to(bias[...], acc.shape)
+    def normed(i):
+        scaled = hid[:, columns(i)].astype(F32) * inverse * gain[:, columns(i)].astype(F32)
+        return scaled.astype(BF16)
+
+    bias = (bias_query, bias_key, bias_value)
+    starts = (0, q_cols, q_cols + HEAD_DIM)
+    for start, part in zip(starts, bias):
+        span = pl.ds(start, part.shape[1])
+        acc[:, span] = jnp.broadcast_to(part[...].astype(F32), (rows, part.shape[1]))
 
     def project(t, carry):
         ring_advance(w_all, w_sems, t)
@@ -168,65 +172,70 @@
         for d in range(2):
             i = 2 * source_at(d, t, core) + d
             k = 2 * source_at(d, t, 1 - core) + d
-            acc[...] += jnp.dot(normed[i], w_all[i], preferred_element_type=F32) + jnp.dot(
-                normed[k], w_all[k], preferred_element_type=F32
+            acc[...] += jnp.dot(normed(i), w_all[i], preferred_element_type=F32) + jnp.dot(
+                normed(k), w_all[k], preferred_element_type=F32
             )
         return carry
 
     lax.fori_loop(0, chips, project, 0)
 
+    block_cos, block_sin = far_cos[me], far_sin[me]
+    cosine = near_cos[...] * block_cos - near_sin[...] * block_sin
+    lane = lax.broadcasted_iota(jnp.int32, cosine.shape, 1)
+    sine = near_sin[...] * block_cos + near_cos[...] * block_sin
+    sine = jnp.where(lane < HEAD_DIM // 2, -sine, sine)
+
     def rotary(x):
-        return x * cosine[...] + pltpu.roll(x, HEAD_DIM // 2, 1) * sine[...]
-
-    kv_all[me, :, pl.ds(0, HEAD_DIM)] = rotary(acc[:, pl.ds(q_cols, HEAD_DIM)]).astype(BF16)
-    kv_all[me, :, pl.ds(HEAD_DIM, HEAD_DIM)] = acc[:, pl.ds(q_cols + HEAD_DIM, HEAD_DIM)].astype(BF16)
+        return x * cosine + pltpu.roll(x, HEAD_DIM // 2, 1) * sine
+
+    def kv_rows(which):
+        return pl.ds(pl.multiple_of(which * rows, rows), rows)
+
+    kv_all[chip, kv_rows(core), pl.ds(0, HEAD_DIM)] = rotary(acc[:, pl.ds(q_cols, HEAD_DIM)]).astype(BF16)
+    kv_all[chip, kv_rows(core), pl.ds(HEAD_DIM, HEAD_DIM)] = acc[:, pl.ds(q_cols + HEAD_DIM, HEAD_DIM)].astype(BF16)
     for h in range(heads):
         q_ref[h] = rotary(acc[:, pl.ds(h * HEAD_DIM, HEAD_DIM)]).astype(BF16)
 
     reach = (chips // 2, chips - 1 - chips // 2)
 
     def kv_copy(owner, ss, rs, direction, step, device):
-        return remote(kv_all.at[owner], ss, rs, direction * chips + step, device)
+        return remote(kv_all.at[owner // 2, kv_rows(owner % 2)], ss, rs, direction * chips + step, device)
 
     for d in range(2):
         kv_copy(me, ks, kr, d, 0, neighbours[d]).start()
     kv_copy(me, kps, kpr, 0, chips - 1, partner).start()
 
-    scaling = HEAD_DIM ** (-0.5)
-
-    def attend(b, first, diagonal):
+    factor = HEAD_DIM ** (-0.5) * 1.4426950408889634
+
+    def attend(c, own):
         for h in range(heads):
             scores = lax.dot_general(
-                q_ref[h], kv_all[b, :, pl.ds(0, HEAD_DIM)], (((1,), (1,)), ((), ())),
+                q_ref[h], kv_all[c, :, pl.ds(0, HEAD_DIM)], (((1,), (1,)), ((), ())),
                 preferred_element_type=F32,
-            ) * scaling
-            if diagonal:
-                row = lax.broadcasted_iota(jnp.int32, scores.shape, 0)
+            )
+            if own:
+                row = lax.broadcasted_iota(jnp.int32, scores.shape, 0) + core * rows
                 col = lax.broadcasted_iota(jnp.int32, scores.shape, 1)
                 scores = jnp.where(row >= col, scores, -jnp.inf)
             top = jnp.max(scores, axis=-1, keepdims=True)
-            if not first:
+            if not own:
                 old = high[h]
                 top = jnp.maximum(old, top)
-            probs = jnp.exp(scores - top)
+            probs = jnp.exp2((scores - top) * factor)
             part = jnp.sum(probs, axis=-1, keepdims=True)
             product = jnp.dot(
-                probs.astype(BF16), kv_all[b, :, pl.ds(HEAD_DIM, HEAD_DIM)], preferred_element_type=F32
+                probs.astype(BF16), kv_all[c, :, pl.ds(HEAD_DIM, HEAD_DIM)], preferred_element_type=F32
             )
-            if not first:
-                shrink = jnp.exp(old - top)
+            if not own:
+                shrink = jnp.exp2((old - top) * factor)
                 part = part + total[h] * shrink
                 product = product + mixed[h] * shrink
             high[h] = top
             total[h] = part
             mixed[h] = product
 
-    attend(me, True, True)
-
-    def attend_earlier(b):
-        @pl.when(b < me)
-        def _():
-            attend(b, False, False)
+    kv_copy(partner, kps, kpr, 0, chips - 1, partner).wait_recv()
+    attend(chip, True)
 
     def attention(t, carry):
         for d in range(2):
@@ -241,22 +250,22 @@
 
                 kv_copy(owner, kps, kpr, d, t, partner).start()
 
-        @pl.when(t == 0)
+        @pl.when(t == reach[0])
         def _():
-            kv_copy(partner, kps, kpr, 0, chips - 1, partner).wait_recv()
-            attend_earlier(partner)
+            ring_begin(wo_all, o_sems)
 
         for d in range(2):
             @pl.when((t > 0) & (t <= reach[d]))
             def _():
-                attend_earlier(source_at(d, t, core))
                 owner = source_at(d, t, 1 - core)
                 kv_copy(owner, kps, kpr, d, t - 1, partner).wait_recv()
-                attend_earlier(owner)
+
+                @pl.when(owner // 2 < chip)
+                def _():
+                    attend(owner // 2, False)
         return carry
 
     lax.fori_loop(0, reach[0] + 1, attention, 0)
-    ring_begin(wo_all, o_sems)
     for h in range(heads):
         att[:, pl.ds(h * HEAD_DIM, HEAD_DIM)] = (mixed[h] / total[h]).astype(BF16)
 
@@ -284,15 +293,6 @@
     def blocks_of(t):
         return [2 * source_at(d, t, which) + d for d in range(2) for which in (core, 1 - core)]
 
-    def project_out(t, carry):
-        ring_advance(wo_all, o_sems, t)
-        partner_wait(wo_all, o_sems, t)
-        for i in blocks_of(t):
-            make_term(i)
-        return carry
-
-    lax.fori_loop(0, chips, project_out, 0)
-
     def finish(t, carry):
         for i in blocks_of(t):
             value = tm[i].astype(F32)
@@ -302,8 +302,23 @@
             out[:, out_columns(i)] = value.astype(BF16)
         return carry
 
+    lag = 3
+
+    def project_out(t, carry):
+        ring_advance(wo_all, o_sems, t)
+        partner_wait(wo_all, o_sems, t)
+        for i in blocks_of(t):
+            make_term(i)
+        if exchange:
+            @pl.when(t >= lag)
+            def _():
+                finish(t - lag, 0)
+        return carry
+
+    lax.fori_loop(0, chips, project_out, 0)
+
     if exchange:
-        lax.fori_loop(0, chips, finish, 0)
+        lax.fori_loop(chips - lag, chips, finish, 0)
 
         def sent(i, carry):
             for p in peers:
@@ -333,15 +348,12 @@
     half_depth = w_query.shape[0] // 2
     half_cols = w_out.shape[1] // 2
 
-    positions = lax.axis_index("seq") * rows + jnp.arange(rows, dtype=jnp.int32)
-    freq = ROPE_BASE ** (-2.0 * jnp.arange(HEAD_DIM // 2, dtype=F32) / HEAD_DIM)
-    angles = positions.astype(F32)[:, None] * freq[None, :]
-    cosine = jnp.cos(angles)
-    sine = jnp.sin(angles)
-    cosine = jnp.concatenate([cosine, cosine], axis=-1)
-    sine = jnp.concatenate([-sine, sine], axis=-1)
-    gain = norm_gain.astype(F32).reshape(slices, 1, width // slices)
-    bias = jnp.concatenate([bias_query, bias_key, bias_value]).astype(F32)[None, :]
+    freq = ROPE_BASE ** (-2.0 * np.arange(HEAD_DIM // 2, dtype=np.float64) / HEAD_DIM)
+    freq = np.concatenate([freq, freq])
+    near = np.arange(rows, dtype=np.float64)[:, None] * freq
+    far = (np.arange(n, dtype=np.float64) * rows)[:, None, None] * freq
+    tables = [f(a).astype(np.float32) for a in (near, far) for f in (np.cos, np.sin)]
+    vectors = [v.reshape(1, -1) for v in (norm_gain, bias_query, bias_key, bias_value)]
 
     any_spec = pl.BlockSpec(memory_space=pl.ANY)
     vmem = pl.BlockSpec(memory_space=pltpu.VMEM)
@@ -352,15 +364,14 @@
     result = pl.pallas_call(
         functools.partial(kernel, n, groups, exchange),
         out_shape=jax.ShapeDtypeStruct((rh if exchange else rows, w_out.shape[1] * n), BF16),
-        in_specs=[any_spec] * 5 + [vmem] * 4,
+        in_specs=[any_spec] * 5 + [vmem] * 8,
         out_specs=vmem,
         scratch_shapes=[
             pltpu.VMEM((rows, width), BF16),
-            pltpu.VMEM((slices, rows, width // slices), BF16),
             pltpu.VMEM((slices, half_depth, wide), BF16),
             pltpu.VMEM((slices, w_out.shape[0], half_cols), BF16),
             pltpu.VMEM((rows, wide), F32),
-            pltpu.VMEM((n, rows, 2 * HEAD_DIM), BF16),
+            pltpu.VMEM((chips, 2 * rows, 2 * HEAD_DIM), BF16),
             pltpu.VMEM((heads, rows, HEAD_DIM), BF16),
             pltpu.VMEM((heads, rows, 1), F32),
             pltpu.VMEM((heads, rows, 1), F32),
@@ -377,7 +388,7 @@
         compiler_params=pltpu.CompilerParams(
             collective_id=0, has_side_effects=True, vmem_limit_bytes=64 * 1024 * 1024 - 128 * 1024
         ),
-    )(hidden, w_query, w_key, w_value, w_out, gain, bias, cosine, sine)
+    )(hidden, w_query, w_key, w_value, w_out, *vectors, *tables)
     if exchange:
         return result
     return lax.psum_scatter(result, "head", scatter_dimension=0, tiled=True)

time: 176 us -> 162 us (0.920)
  Pallas kernels: 168 us -> 156 us
  other arithmetic: 4.06 us -> 0 us
  local copies, waits for them, and re-layouts: 3.96 us -> 5.9 us
    pallas_call x1, Pallas kernels: 168 us -> 156 us  [local(): pl.pallas_call(functools.partial(kernel, n, groups, exchange), out_shape=...]
    reshape x0 -> x2, local copies, waits for them, and re-layouts: none -> 2.62 us  [local(): v.reshape(1, -1)]
where the time goes in v2:
time: 162 us
  Pallas kernels  156 us (96%)
  local copies, waits for them, and re-layouts  5.9 us (4%)
    pallas_call x1, Pallas kernels, local(): pl.pallas_call(functools.partial(kernel, n, groups, exchange), out_shape=...  156 us
    unnamed x1, local copies, waits for them, and re-layouts  3.27 us

profile of v2, /device:TPU:18, one launch (start us, length us, event | category | flops | bytes accessed | tf_op | source)
XLA Modules:
  0.0 161.6 jit_solution(8714640967746855594)
XLA Ops:
  0.0 1.3 reshape.13.bias_query
  1.3 1.3 reshape.12.gain
  2.6 155.7 %shard_map.127 = bf16[144,8192]{1,0:T(8,128)(2,1)} custom-call(bf16[288,8192]{1,0:T(8,128)(2,1)} %hidden.1, bf16[512,512]{1,0:T(8,128)(2,1)} %w_query.1, bf16[512,128]{1,0:T(8,128)(2,1)} %w_key.1, bf16[512,128]{1,0:T(8,128)(2,1)} %w_value.1, bf16[512,512]{1,0:T(8,128)(2,1)} %w_out.1, bf16[1,8192]{1,0:T(2,128)(2,1)} %reshape.12.gain, ...), custom_call_target="tpu_custom_call" | custom-call | tf_op jit(solution)/shard_map/pallas_call | solution.py:364
  158.3 3.3 %copy.15 = bf16[144,8192]{1,0:T(8,128)(2,1)} copy(bf16[144,8192]{1,0:T(8,128)(2,1)} %shard_map.127) | data formatting | bytes 4718592

commit v3 on v2

--- a/solution.py
+++ b/solution.py
@@ -53,15 +53,16 @@
     half_cols = w_out.shape[1] // 2
     rh = rows // groups
 
-    loads = [pltpu.make_async_copy(hidden, hid, load_sem.at[0])]
+    loads = []
+    late = [pltpu.make_async_copy(hidden, hid, load_sem.at[0])]
     for h in range(2):
         span = pl.ds(h * half_depth, half_depth)
         slot = w_all.at[2 * me + h]
         loads.append(pltpu.make_async_copy(w_query.at[span], slot.at[:, pl.ds(0, q_cols)], load_sem.at[1 + 4 * h]))
         loads.append(pltpu.make_async_copy(w_key.at[span], slot.at[:, pl.ds(q_cols, HEAD_DIM)], load_sem.at[2 + 4 * h]))
         loads.append(pltpu.make_async_copy(w_value.at[span], slot.at[:, pl.ds(q_cols + HEAD_DIM, HEAD_DIM)], load_sem.at[3 + 4 * h]))
-        loads.append(pltpu.make_async_copy(w_out.at[:, pl.ds(h * half_cols, half_cols)], wo_all.at[2 * me + h], load_sem.at[4 + 4 * h]))
-    for copy in loads:
+        late.append(pltpu.make_async_copy(w_out.at[:, pl.ds(h * half_cols, half_cols)], wo_all.at[2 * me + h], load_sem.at[4 + 4 * h]))
+    for copy in loads + late:
         copy.start()
 
     barrier = pltpu.get_barrier_semaphore()
@@ -139,10 +140,11 @@
     w_sems = (ws, wr, wps, wpr)
     o_sems = (os_, or_, ops, opr)
 
-    for copy in loads[1:]:
+    for copy in loads:
         copy.wait()
     ring_begin(w_all, w_sems)
-    loads[0].wait()
+    for copy in late:
+        copy.wait()
     slices = 2 * n
     step_cols = width // slices
 
@@ -198,12 +200,18 @@
 
     reach = (chips // 2, chips - 1 - chips // 2)
 
-    def kv_copy(owner, ss, rs, direction, step, device):
-        return remote(kv_all.at[owner // 2, kv_rows(owner % 2)], ss, rs, direction * chips + step, device)
-
-    for d in range(2):
-        kv_copy(me, ks, kr, d, 0, neighbours[d]).start()
-    kv_copy(me, kps, kpr, 0, chips - 1, partner).start()
+    parts = 2 if rows % 32 == 0 else 1
+    piece_rows = rows // parts
+
+    def kv_copy(owner, ss, rs, direction, step, j, device):
+        start = pl.multiple_of((owner % 2) * rows + j * piece_rows, piece_rows)
+        block = kv_all.at[owner // 2, pl.ds(start, piece_rows)]
+        return remote(block, ss, rs, key_of(direction, step, j), device)
+
+    for j in range(parts):
+        for d in range(2):
+            kv_copy(me, ks, kr, d, 0, j, neighbours[d]).start()
+        kv_copy(me, kps, kpr, 0, chips - 1, j, partner).start()
 
     factor = HEAD_DIM ** (-0.5) * 1.4426950408889634
 
@@ -234,21 +242,23 @@
             total[h] = part
             mixed[h] = product
 
-    kv_copy(partner, kps, kpr, 0, chips - 1, partner).wait_recv()
+    for j in range(parts):
+        kv_copy(partner, kps, kpr, 0, chips - 1, j, partner).wait_recv()
     attend(chip, True)
 
     def attention(t, carry):
-        for d in range(2):
-            @pl.when(t < reach[d])
-            def _():
-                owner = source_at(d, t + 1, core)
-                kv_copy(owner, ks, kr, d, t, neighbours[d]).wait_recv()
-
-                @pl.when(t + 1 < reach[d])
+        for j in range(parts):
+            for d in range(2):
+                @pl.when(t < reach[d])
                 def _():
-                    kv_copy(owner, ks, kr, d, t + 1, neighbours[d]).start()
-
-                kv_copy(owner, kps, kpr, d, t, partner).start()
+                    owner = source_at(d, t + 1, core)
+                    kv_copy(owner, ks, kr, d, t, j, neighbours[d]).wait_recv()
+
+                    @pl.when(t + 1 < reach[d])
+                    def _():
+                        kv_copy(owner, ks, kr, d, t + 1, j, neighbours[d]).start()
+
+                    kv_copy(owner, kps, kpr, d, t, j, partner).start()
 
         @pl.when(t == reach[0])
         def _():
@@ -258,7 +268,8 @@
             @pl.when((t > 0) & (t <= reach[d]))
             def _():
                 owner = source_at(d, t, 1 - core)
-                kv_copy(owner, kps, kpr, d, t - 1, partner).wait_recv()
+                for j in range(parts):
+                    kv_copy(owner, kps, kpr, d, t - 1, j, partner).wait_recv()
 
                 @pl.when(owner // 2 < chip)
                 def _():
@@ -329,11 +340,12 @@
 
     ring_drain(w_all, w_sems)
     ring_drain(wo_all, o_sems)
-    for d in range(2):
-        for t in range(reach[d]):
-            kv_copy(me, ks, kr, d, t, neighbours[d]).wait_send()
-            kv_copy(me, kps, kpr, d, t, partner).wait_send()
-    kv_copy(me, kps, kpr, 0, chips - 1, partner).wait_send()
+    for j in range(parts):
+        for d in range(2):
+            for t in range(reach[d]):
+                kv_copy(me, ks, kr, d, t, j, neighbours[d]).wait_send()
+                kv_copy(me, kps, kpr, d, t, j, partner).wait_send()
+        kv_copy(me, kps, kpr, 0, chips - 1, j, partner).wait_send()
 
 
 def local(n, groups, hidden, norm_gain, w_query, w_key, w_value, bias_query, bias_key, bias_value, w_out):
@@ -382,8 +394,7 @@
             pltpu.VMEM((pieces, rpart, half_cols), BF16),
             dma((9,)),
         ]
-        + [dma((4 * chips,))] * 8
-        + [dma((2 * chips,))] * 4
+        + [dma((4 * chips,))] * 12
         + [dma((links * pieces,))] * 2,
         compiler_params=pltpu.CompilerParams(
             collective_id=0, has_side_effects=True, vmem_limit_bytes=64 * 1024 * 1024 - 128 * 1024

time: 162 us -> 160 us (0.988)
  Pallas kernels: 156 us -> 154 us
    pallas_call x1, Pallas kernels: 156 us -> 154 us  [local(): pl.pallas_call(functools.partial(kernel, n, groups, exchange), out_shape=...]
where the time goes in v3:
time: 160 us
  Pallas kernels  154 us (96%)
  local copies, waits for them, and re-layouts  5.9 us (4%)
    pallas_call x1, Pallas kernels, local(): pl.pallas_call(functools.partial(kernel, n, groups, exchange), out_shape=...  154 us
    unnamed x1, local copies, waits for them, and re-layouts  3.27 us

profile of v3, /device:TPU:18, one launch (start us, length us, event | category | flops | bytes accessed | tf_op | source)
XLA Modules:
  0.0 159.7 jit_solution(9139860615299696985)
XLA Ops:
  0.0 1.3 reshape.13.bias_query
  1.3 1.3 reshape.12.gain
  2.6 153.8 %shard_map.127 = bf16[144,8192]{1,0:T(8,128)(2,1)} custom-call(bf16[288,8192]{1,0:T(8,128)(2,1)} %hidden.1, bf16[512,512]{1,0:T(8,128)(2,1)} %w_query.1, bf16[512,128]{1,0:T(8,128)(2,1)} %w_key.1, bf16[512,128]{1,0:T(8,128)(2,1)} %w_value.1, bf16[512,512]{1,0:T(8,128)(2,1)} %w_out.1, bf16[1,8192]{1,0:T(2,128)(2,1)} %reshape.12.gain, ...), custom_call_target="tpu_custom_call" | custom-call | tf_op jit(solution)/shard_map/pallas_call | solution.py:376
  156.4 3.3 %copy.15 = bf16[144,8192]{1,0:T(8,128)(2,1)} copy(bf16[144,8192]{1,0:T(8,128)(2,1)} %shard_map.127) | data formatting | bytes 4718592

commit v4 on v3

--- a/solution.py
+++ b/solution.py
@@ -260,7 +260,7 @@
 
                     kv_copy(owner, kps, kpr, d, t, j, partner).start()
 
-        @pl.when(t == reach[0])
+        @pl.when(t == reach[0] - 1)
         def _():
             ring_begin(wo_all, o_sems)
 
@@ -315,11 +315,27 @@
 
     lag = 3
 
+    def partner_terms(t):
+        partner_wait(wo_all, o_sems, t)
+        for d in range(2):
+            make_term(2 * source_at(d, t, 1 - core) + d)
+
+    for d in range(2):
+        make_term(2 * me + d)
+    partner_terms(0)
+
     def project_out(t, carry):
         ring_advance(wo_all, o_sems, t)
-        partner_wait(wo_all, o_sems, t)
-        for i in blocks_of(t):
-            make_term(i)
+
+        @pl.when(t < chips - 1)
+        def _():
+            for d in range(2):
+                make_term(2 * source_at(d, t + 1, core) + d)
+
+        @pl.when(t > 0)
+        def _():
+            partner_terms(t)
+
         if exchange:
             @pl.when(t >= lag)
             def _():

time: 160 us -> 156 us (0.975)
  Pallas kernels: 154 us -> 149 us
    pallas_call x1, Pallas kernels: 154 us -> 149 us  [local(): pl.pallas_call(functools.partial(kernel, n, groups, exchange), out_shape=...]
where the time goes in v4:
time: 156 us; the launch traced here: 155 us
  Pallas kernels  149 us (96%)
  local copies, waits for them, and re-layouts  5.9 us (4%)
    pallas_call x1, Pallas kernels, local(): pl.pallas_call(functools.partial(kernel, n, groups, exchange), out_shape=...  149 us
    unnamed x1, local copies, waits for them, and re-layouts  3.27 us

profile of v4, /device:TPU:18, one launch (start us, length us, event | category | flops | bytes accessed | tf_op | source)
XLA Modules:
  0.0 154.8 jit_solution(10032460355386758714)
XLA Ops:
  0.0 1.3 reshape.13.bias_query
  1.3 1.3 reshape.12.gain
  2.6 148.9 %shard_map.127 = bf16[144,8192]{1,0:T(8,128)(2,1)} custom-call(bf16[288,8192]{1,0:T(8,128)(2,1)} %hidden.1, bf16[512,512]{1,0:T(8,128)(2,1)} %w_query.1, bf16[512,128]{1,0:T(8,128)(2,1)} %w_key.1, bf16[512,128]{1,0:T(8,128)(2,1)} %w_value.1, bf16[512,512]{1,0:T(8,128)(2,1)} %w_out.1, bf16[1,8192]{1,0:T(2,128)(2,1)} %reshape.12.gain, ...), custom_call_target="tpu_custom_call" | custom-call | tf_op jit(solution)/shard_map/pallas_call | solution.py:392
  151.5 3.3 %copy.15 = bf16[144,8192]{1,0:T(8,128)(2,1)} copy(bf16[144,8192]{1,0:T(8,128)(2,1)} %shard_map.127) | data formatting | bytes 4718592
